TPU v7x, 32 devices: a whole 2x2x4 slice. The times are simulated.
32 devices in a mesh: param: 16 (over z, x, core), qoi: 2 (over y).
Axes of the slice: x: 2, y: 2, z: 4, core: 2. Of those that a mesh axis runs over, the one named last changes fastest.
Arguments:
- samples: bfloat16 [16, 5120, 420], P('qoi', 'param'), may hold values from -6 to 6
- operator_rows: bfloat16 [8, 5120, 2, 512], P(None, 'param', None, 'qoi'), may hold values from -0.0625 to 0.0625
- block_start: int32 [1], replicated, may hold values from 0 to 203
- gauge_group: int32 [512], P('qoi'), may hold values from 0 to 15
Outputs:
- qoi_spectrum: float32 [16, 2, 8, 512], P('param', None, None, 'qoi')
- segment_response: float32 [16, 2, 8, 16], P('param')
Inputs may be any that keep to these rules, and one draw needn't show every extreme that they name: `block_start`: the block's frequencies lie among the 211 frequencies of a real transform.
All inputs are finite; a program needn't handle non-finite values.
Results may differ from a plain program's by a relative error of at most 0.005.
Values may be sent and summed in bfloat16 or wider, within the bound.
A program may use at most 64 MiB of HBM per device.

v0:
```python
import math

import jax
import jax.numpy as jnp
from jax import lax
from jax.sharding import PartitionSpec as P

GROUPS = 16


def build_table(block_start, steps_count, freq_count):
    time_index = jnp.arange(steps_count, dtype=jnp.int32)
    freq_index = block_start[0] + jnp.arange(freq_count, dtype=jnp.int32)
    phase_index = time_index[:, None] * freq_index[None, :] % steps_count
    phases = phase_index.astype(jnp.float32) * (2.0 * math.pi / steps_count)
    table = jnp.concatenate([jnp.cos(phases), -jnp.sin(phases)], axis=1) / math.sqrt(steps_count)
    table_high = lax.optimization_barrier(table.astype(jnp.bfloat16))
    table_low = (table - table_high.astype(jnp.float32)).astype(jnp.bfloat16)
    return jnp.concatenate([table_high, table_low], axis=1)


def transform(series, combined, freq_count):
    sample_count, param_local, steps_count = series.shape
    flat = series.reshape(sample_count * param_local, steps_count)
    halves = jnp.dot(flat, combined, preferred_element_type=jnp.float32)
    spectrum = (halves[:, : 2 * freq_count] + halves[:, 2 * freq_count :]).astype(jnp.bfloat16)
    return spectrum.reshape(sample_count, param_local, 2, freq_count).transpose(3, 2, 0, 1)


def local(samples, operator_rows, block_start, gauge_group):
    freq_count = operator_rows.shape[0]
    param_local = operator_rows.shape[1]
    gauge_local = operator_rows.shape[3]
    combined = build_table(block_start, samples.shape[2], freq_count)
    spectra = lax.all_gather(transform(samples, combined, freq_count), "qoi", axis=2, tiled=True)
    sample_total = spectra.shape[2]
    weights = operator_rows.reshape(freq_count, param_local, 2 * gauge_local)
    param_count = lax.axis_size("param")
    own_rows = sample_total // param_count
    product = jnp.einsum("fkcp,fpx->ckfx", spectra, weights, preferred_element_type=jnp.float32)
    real_part = product[:, 0, :, :gauge_local] - product[:, 1, :, gauge_local:]
    imag_part = product[:, 0, :, gauge_local:] + product[:, 1, :, :gauge_local]
    all_terms = jnp.stack([real_part, imag_part], axis=1)
    received = lax.all_to_all(
        all_terms.astype(jnp.bfloat16), "param", split_axis=0, concat_axis=0, tiled=True
    ).astype(all_terms.dtype)
    qoi_spectrum = jnp.sum(
        received.reshape(param_count, own_rows, 2, freq_count, gauge_local), axis=0
    )
    onehot = (gauge_group[:, None] == jnp.arange(GROUPS, dtype=jnp.int32)[None, :]).astype(
        jnp.float32
    )
    local_sums = jnp.dot(
        qoi_spectrum.reshape(-1, gauge_local),
        onehot,
        precision=lax.Precision.HIGHEST,
        preferred_element_type=jnp.float32,
    )
    local_sums = local_sums.reshape(own_rows, 2, freq_count, GROUPS)
    summed = lax.psum(local_sums, "qoi")
    norm_factor = math.sqrt(GROUPS / (gauge_local * lax.axis_size("qoi")))
    return (qoi_spectrum, summed * norm_factor)


def solution(mesh):
    return jax.shard_map(
        local,
        mesh=mesh,
        in_specs=(P("qoi", "param", None), P(None, "param", None, "qoi"), P(), P("qoi")),
        out_specs=(P("param", None, None, "qoi"), P("param", None, None, None)),
        check_vma=False,
    )
```

profile of v0, /device:TPU:0, one launch (start us, length us, event | category | flops | bytes accessed | tf_op | source)
XLA Modules:
  0.0 37.9 jit_solution(8787217125666526188)
XLA Ops:
  1.3 0.2 fusion.16
  1.5 4.1 %reshape.28 = bf16[2560,420]{0,1:T(8,128)(2,1)S(1)} reshape(bf16[8,320,420]{1,0,2:T(8,128)(2,1)} %param.4) | data formatting | bytes 4300800 | tf_op jit(solution)/shard_map/reshape | solution.py:24
  5.6 0.5 %convolution_bitcast_fusion = f32[2560,32]{0,1:T(8,128)S(1)} fusion(bf16[2560,420]{0,1:T(8,128)(2,1)S(1)} %reshape.28, bf16[420,16]{0,1:T(8,128)(2,1)S(1)} %subtract_convert_fusion, bf16[420,16]{0,1:T(8,128)(2,1)S(1)} %fusion.11), kind=kOutput, calls=%fused_computation | convolution fusion | flops 68866560 | bytes 2504960 | tf_op jit(solution)/shard_map/dot_general | solution.py:25
  6.1 0.1 reshape.29
  6.2 6.5 %all_gather.3 = bf16[8,2,16,320]{3,2,1,0:T(8,128)(2,1)S(1)} all-gather(bf16[8,2,8,320]{3,2,1,0:T(8,128)(2,1)S(1)} %bitcast.29), channel_id=1, replica_groups=mesh['param'=16,'qoi'=2] {'qoi'}, dimensions={2}, use_global_device_ids=true | all-gather | bytes 245760 | tf_op jit(solution)/shard_map/all_gather | solution.py:35
  12.7 4.2 %reshape.31 = bf16[8,320,512,1]{2,1,0,3:T(8,128)(2,1)S(1)} reshape(bf16[8,320,2,256]{3,2,1,0:T(2,128)(2,1)} %param.5) | data formatting | bytes 5242880 | tf_op jit(solution)/shard_map/reshape | solution.py:37
  16.9 0.0 copy-start
  16.9 0.5 %fusion.2 = f32[16,2,8,512]{3,0,1,2:T(8,128)S(1)} fusion(bf16[8,2,16,320]{3,2,1,0:T(8,128)(2,1)S(1)} %all_gather.3, bf16[8,320,512,1]{2,1,0,3:T(8,128)(2,1)S(1)} %reshape.31), kind=kOutput, calls=%fused_computation.3 | convolution fusion | flops 83886080 | bytes 3309568 | tf_op jit(solution)/shard_map/fkcp,fpx->ckfx/dot_general | solution.py:40
  17.5 0.1 copy.13
  17.6 13.9 %all_to_all.5 = bf16[16,2,8,256]{3,1,2,0:T(2,128)(2,1)S(1)} all-to-all(bf16[16,2,8,256]{3,1,2,0:T(2,128)(2,1)S(1)} %copy.13), channel_id=1, replica_groups=mesh['param'=16,'qoi'=2] {'param'}, dimensions={0} | all-to-all | bytes 262144 | tf_op jit(solution)/shard_map/all_to_all | solution.py:44
  31.6 0.0 copy-done
  31.6 0.1 convolution_bitcast_fusion.1
  31.7 0.6 %copy.17 = f32[1,2,8,256]{3,2,1,0:T(8,128)} copy(f32[1,2,8,256]{3,1,2,0:T(2,128)S(1)} %bitcast.30) | data formatting | bytes 32768
  32.3 5.0 %psum.7 = f32[1,2,8,16]{3,2,1,0:T(8,128)S(1)} all-reduce(f32[1,2,8,16]{3,2,1,0:T(8,128)S(1)} %convolution_bitcast_fusion.1), channel_id=1, replica_groups=mesh['param'=16,'qoi'=2] {'qoi'}, use_global_device_ids=true, to_apply=%region_1.2 | all-reduce | flops 256 | bytes 2048 | tf_op jit(solution)/shard_map/psum | solution.py:60
  37.3 0.6 %broadcast_multiply_fusion = f32[1,2,8,16]{3,2,1,0:T(8,128)} fusion(f32[1,2,8,16]{3,2,1,0:T(8,128)S(1)} %psum.7), kind=kLoop, calls=%fused_computation.33 | loop fusion | flops 256 | bytes 2048 | tf_op jit(solution)/shard_map/mul | solution.py:62
  (9 shorter events, 0.1 us)
Async XLA Ops:
  16.9 14.7 %copy-start = (s32[256]{0:T(256)S(1)}, s32[256]{0:T(256)}, u32[]{:S(2)}) copy-start(s32[256]{0:T(256)} %param.7) | copy-start | bytes 3076
where the time goes:
time: 38.2 us; the launch traced here: 37.9 us
  blocking collectives  25.3 us (66%)
  local copies, waits for them, and re-layouts  9.13 us (24%)
  between operations  1.38 us (4%)
  matrix products  1.14 us (3%)
  other arithmetic  0.88 us (2%)
    all_to_all x1, blocking collectives, local(): lax.all_to_all(all_terms.astype(jnp.bfloat16), 'param', split_axis=0, con...  13.9 us
    all_gather x1, blocking collectives, local(): lax.all_gather(transform(samples, combined, freq_count), 'qoi', axis=2, t...  6.46 us
    psum x1, blocking collectives, local(): summed = lax.psum(local_sums, 'qoi')  4.96 us
    reshape x1, local copies, waits for them, and re-layouts, local(): weights = operator_rows.reshape(freq_count, param_local, 2 * gauge_local)  4.16 us
    reshape x1, local copies, waits for them, and re-layouts, transform(): flat = series.reshape(sample_count * param_local, steps_count)  4.09 us

commit v1 on v0

v1 whole, which is shorter than its diff:
```python
import functools
import math

import jax
import jax.numpy as jnp
from jax import lax
from jax.experimental import pallas as pl
from jax.experimental.pallas import tpu as pltpu
from jax.sharding import PartitionSpec as P

GROUPS = 16
LANES = 128
CHUNKS = 2
PARTS = 2
MESH = pl.DeviceIdType.MESH
NT_DIMS = (((1,), (1,)), ((), ()))


def build_table(start, freq_count, steps_count, first, count, repeat):
    shape = (freq_count, count * repeat)
    steps = first + lax.broadcasted_iota(jnp.int32, shape, 1) // repeat
    freqs = lax.broadcasted_iota(jnp.int32, shape, 0) + start
    turns = (steps * freqs).astype(jnp.float32)
    whole = jnp.floor((turns + 0.5) * (1.0 / steps_count))
    phases = (turns - whole * steps_count) * (2.0 * math.pi / steps_count)
    table = jnp.concatenate([jnp.cos(phases), -jnp.sin(phases)], axis=0) * (
        1.0 / math.sqrt(steps_count)
    )
    high = table.astype(jnp.bfloat16).astype(jnp.float32)
    both = jnp.concatenate([high, table - high], axis=0)
    full = (4 * freq_count, repeat, count * repeat)
    keep = lax.broadcasted_iota(jnp.int32, full, 2) % repeat == lax.broadcasted_iota(
        jnp.int32, full, 1
    )
    wide = jnp.where(keep, both[:, None, :], 0.0)
    return wide.reshape(4 * freq_count * repeat, count * repeat).astype(jnp.bfloat16)


def spread(width):
    row = lax.broadcasted_iota(jnp.int32, (2 * width, 2 * width), 0)
    col = lax.broadcasted_iota(jnp.int32, (2 * width, 2 * width), 1)
    real = jnp.where(col == 2 * row, 1.0, 0.0)
    imag = jnp.where(col == 2 * (row - width) + 1, -1.0, 0.0)
    return jnp.where(row < width, real, imag).astype(jnp.bfloat16)


def swap():
    row = lax.broadcasted_iota(jnp.int32, (LANES, LANES), 0)
    col = lax.broadcasted_iota(jnp.int32, (LANES, LANES), 1)
    odd = col % 2
    value = jnp.where(odd == 1, 1.0, -1.0)
    return jnp.where(row == col + 1 - 2 * odd, value, 0.0).astype(jnp.bfloat16)


def kernel(
    param_count, qoi_count, start_hbm, group_ref, samples_hbm, rows_hbm,
    out_ref, seg_ref,
    start_ref, samples, weights, line, product, outgoing, incoming, total, segments,
    start_sem, samples_sem, weights_sem, line_send, line_recv, out_send, out_recv, seg_send, seg_recv,
):
    steps_count, sample_local, param_local = samples.shape
    freq_count, halves = weights.shape[0], weights.shape[1]
    gauge_local = halves * LANES
    sample_total = sample_local * qoi_count
    depth = 2 * param_local
    per_chunk = freq_count // CHUNKS
    me_p = lax.axis_index("param")
    me_q = lax.axis_index("qoi")

    barrier = pltpu.get_barrier_semaphore()
    for offset in range(1, qoi_count):
        pl.semaphore_signal(
            barrier, inc=1, device_id=(me_p, lax.rem(me_q + offset, qoi_count)), device_id_type=MESH
        )
    for offset in range(1, param_count):
        pl.semaphore_signal(
            barrier, inc=1, device_id=(lax.rem(me_p + offset, param_count), me_q), device_id_type=MESH
        )

    start_copy = pltpu.make_async_copy(start_hbm, start_ref, start_sem)
    start_copy.start()
    edges = [steps_count * part // PARTS // 32 * 32 for part in range(PARTS)] + [steps_count]
    sample_copies = []
    for part in range(PARTS):
        picked = pl.ds(edges[part], edges[part + 1] - edges[part])
        copy = pltpu.make_async_copy(
            samples_hbm.at[picked], samples.at[picked], samples_sem.at[part]
        )
        copy.start()
        sample_copies.append(copy)
    weight_copies = []
    for f in range(freq_count):
        for j in range(halves):
            copy = pltpu.make_async_copy(
                rows_hbm.at[f, :, :, pl.ds(j * LANES, LANES)],
                weights.at[f, j],
                weights_sem.at[f, j],
            )
            copy.start()
            weight_copies.append(copy)

    start_copy.wait()
    start = start_ref[0]
    swapper = swap()
    both = None
    for part in range(PARTS):
        first, count = edges[part], edges[part + 1] - edges[part]
        table = build_table(start, freq_count, steps_count, first, count, sample_local)
        sample_copies[part].wait()
        block = samples[pl.ds(first, count)].reshape(count * sample_local, param_local)
        term = jnp.dot(table, block, preferred_element_type=jnp.float32)
        both = term if both is None else both + term
    half = 2 * freq_count * sample_local
    spectrum = (both[:half] + both[half:]).astype(jnp.bfloat16)
    blocks = depth // LANES
    for base in range(0, param_local, LANES):
        width = min(LANES, param_local - base)
        pair = jnp.concatenate(
            [spectrum[: half // 2, base : base + width], spectrum[half // 2 :, base : base + width]],
            axis=1,
        )
        value = jnp.dot(pair, spread(width), preferred_element_type=jnp.float32)
        line[0, :, :, 2 * base : 2 * (base + width)] = (
            value.reshape(freq_count, sample_local, 2 * width).astype(jnp.bfloat16)
        )

    pl.semaphore_wait(barrier, qoi_count + param_count - 2)
    line_copies = []
    for chunk in range(CHUNKS):
        picked = pl.ds(chunk * per_chunk, per_chunk)
        for offset in range(1, qoi_count):
            copy = pltpu.make_async_remote_copy(
                src_ref=line.at[0, picked],
                dst_ref=line.at[offset, picked],
                send_sem=line_send.at[chunk, offset],
                recv_sem=line_recv.at[chunk, offset],
                device_id=(me_p, lax.rem(me_q + offset, qoi_count)),
                device_id_type=MESH,
            )
            copy.start()
            line_copies.append(copy)

    out_copies = []
    stripe = 2 * per_chunk
    for chunk in range(CHUNKS):
        for offset in range(1, qoi_count):
            line_copies[chunk * (qoi_count - 1) + offset - 1].wait_recv()
        for f in range(chunk * per_chunk, (chunk + 1) * per_chunk):
            real = jnp.concatenate([line[slot, f] for slot in range(qoi_count)], axis=0)
            stacked = jnp.concatenate(
                [real[:, b * LANES : (b + 1) * LANES] for b in range(blocks)], axis=0
            )
            turned = jnp.dot(stacked, swapper, preferred_element_type=jnp.float32).astype(
                jnp.bfloat16
            )
            imag = jnp.concatenate(
                [turned[b * sample_total : (b + 1) * sample_total] for b in range(blocks)], axis=1
            )
            left = jnp.concatenate([real, imag], axis=0)
            for j in range(halves):
                weight_copies[f * halves + j].wait()
            right = jnp.concatenate(
                [weights[f, j].reshape(depth, LANES) for j in range(halves)], axis=1
            )
            result = jnp.dot(left, right, preferred_element_type=jnp.float32)
            for j in range(halves):
                product[j, pl.ds(f * 2 * sample_total, 2 * sample_total), :] = result[
                    :, j * LANES : (j + 1) * LANES
                ]
        for r in range(sample_total):
            for j in range(halves):
                outgoing[r, chunk, :, j * LANES : (j + 1) * LANES] = product[
                    j,
                    pl.ds(chunk * per_chunk * 2 * sample_total + r, stripe, stride=sample_total),
                    :,
                ].astype(jnp.bfloat16)
        for offset in range(1, param_count):
            target = lax.rem(me_p + offset, param_count)
            slot = lax.rem(me_q + qoi_count - target // sample_local, qoi_count)
            place = slot * sample_local + lax.rem(target, sample_local)
            copy = pltpu.make_async_remote_copy(
                src_ref=outgoing.at[place, chunk],
                dst_ref=incoming.at[offset, chunk],
                send_sem=out_send.at[chunk, offset],
                recv_sem=out_recv.at[chunk, offset],
                device_id=(target, me_q),
                device_id_type=MESH,
            )
            copy.start()
            out_copies.append(copy)

    group_rows = lax.broadcasted_iota(jnp.int32, (LANES, gauge_local), 0)
    onehot = (group_rows == group_ref[...]).astype(jnp.float32)
    slot = lax.rem(me_q + qoi_count - me_p // sample_local, qoi_count)
    place = slot * sample_local + lax.rem(me_p, sample_local)
    for chunk in range(CHUNKS):
        partial = outgoing[place, chunk].astype(jnp.float32)
        for offset in range(1, param_count):
            out_copies[chunk * (param_count - 1) + offset - 1].wait_recv()
            partial = partial + incoming[offset, chunk].astype(jnp.float32)
        for j in range(halves):
            total[j, pl.ds(chunk * stripe, stripe), :] = partial[:, j * LANES : (j + 1) * LANES]
    ordered = jnp.concatenate(
        [
            jnp.concatenate(
                [total[j, pl.ds(part, freq_count, stride=2), :] for j in range(halves)], axis=1
            )
            for part in range(2)
        ],
        axis=0,
    )
    sums = lax.dot_general(
        ordered, onehot, NT_DIMS, precision=lax.Precision.HIGHEST,
        preferred_element_type=jnp.float32,
    )
    segments[me_q] = sums
    seg_copies = []
    for offset in range(1, qoi_count):
        copy = pltpu.make_async_remote_copy(
            src_ref=segments.at[me_q],
            dst_ref=segments.at[me_q],
            send_sem=seg_send.at[offset],
            recv_sem=seg_recv.at[offset],
            device_id=(me_p, lax.rem(me_q + offset, qoi_count)),
            device_id_type=MESH,
        )
        copy.start()
        seg_copies.append(copy)
    out_ref[...] = ordered.reshape(out_ref.shape)
    for copy in line_copies + out_copies:
        copy.wait_send()
    for copy in seg_copies:
        copy.wait()
    everything = segments[0]
    for q in range(1, qoi_count):
        everything = everything + segments[q]
    everything = everything * math.sqrt(GROUPS / (gauge_local * qoi_count))
    seg_ref[...] = everything[:, :GROUPS].reshape(seg_ref.shape)


def local(samples, operator_rows, block_start, gauge_group):
    sample_local, param_local, steps_count = samples.shape
    freq_count, _, _, gauge_local = operator_rows.shape
    param_count, qoi_count = lax.axis_size("param"), lax.axis_size("qoi")
    sample_total = sample_local * qoi_count
    halves = gauge_local // LANES
    depth = 2 * param_local
    stripe = 2 * freq_count // CHUNKS
    assert sample_total == param_count
    dma = pltpu.SemaphoreType.DMA
    vmem = pl.BlockSpec(memory_space=pltpu.VMEM)
    return pl.pallas_call(
        functools.partial(kernel, param_count, qoi_count),
        out_shape=(
            jax.ShapeDtypeStruct((1, 2, freq_count, gauge_local), jnp.float32),
            jax.ShapeDtypeStruct((1, 2, freq_count, GROUPS), jnp.float32),
        ),
        in_specs=[
            pl.BlockSpec(memory_space=pl.ANY),
            vmem,
            pl.BlockSpec(memory_space=pl.ANY),
            pl.BlockSpec(memory_space=pl.ANY),
        ],
        out_specs=(vmem, vmem),
        scratch_shapes=[
            pltpu.SMEM((1,), jnp.int32),
            pltpu.VMEM((steps_count, sample_local, param_local), jnp.bfloat16),
            pltpu.VMEM((freq_count, halves, param_local, 2, LANES), jnp.bfloat16),
            pltpu.VMEM((qoi_count, freq_count, sample_local, depth), jnp.bfloat16),
            pltpu.VMEM((halves, freq_count * 2 * sample_total, LANES), jnp.float32),
            pltpu.VMEM((sample_total, CHUNKS, stripe, gauge_local), jnp.bfloat16),
            pltpu.VMEM((param_count, CHUNKS, stripe, gauge_local), jnp.bfloat16),
            pltpu.VMEM((halves, 2 * freq_count, LANES), jnp.float32),
            pltpu.VMEM((qoi_count, 2 * freq_count, LANES), jnp.float32),
            dma(()),
            dma((PARTS,)),
            dma((freq_count, halves)),
            dma((CHUNKS, qoi_count)),
            dma((CHUNKS, qoi_count)),
            dma((CHUNKS, param_count)),
            dma((CHUNKS, param_count)),
            dma((qoi_count,)),
            dma((qoi_count,)),
        ],
        compiler_params=pltpu.CompilerParams(collective_id=0, has_side_effects=True),
    )(block_start, gauge_group.reshape(1, gauge_local), samples.transpose(2, 0, 1), operator_rows)


def solution(mesh):
    return jax.shard_map(
        local,
        mesh=mesh,
        in_specs=(P("qoi", "param", None), P(None, "param", None, "qoi"), P(), P("qoi")),
        out_specs=(P("param", None, None, "qoi"), P("param", None, None, None)),
        check_vma=False,
    )
```

time: 38.2 us -> 26.6 us (0.70)
  blocking collectives: 25.3 us -> 0 us
  Pallas kernels: 0 us -> 22.3 us
  local copies, waits for them, and re-layouts: 9.13 us -> 2.62 us
  matrix products: 1.14 us -> 0 us
  other arithmetic: 0.88 us -> 0 us
    pallas_call x0 -> x1, Pallas kernels: none -> 22.3 us  [local(): pl.pallas_call(functools.partial(kernel, param_count, qoi_count), out_sha...]
    all_to_all x1 -> x0, blocking collectives: 13.9 us -> none  [local(): lax.all_to_all(all_terms.astype(jnp.bfloat16), 'param', split_axis=0, con...]
    reshape x4 -> x0, local copies, waits for them, and re-layouts: 8.39 us -> none  [the longest x1 4.16 us: local(): weights = operator_rows.reshape(freq_count, param_local, 2 * gauge_local)]
    all_gather x1 -> x0, blocking collectives: 6.46 us -> none  [local(): lax.all_gather(transform(samples, combined, freq_count), 'qoi', axis=2, t...]
    psum x1 -> x0, blocking collectives: 4.96 us -> none  [local(): summed = lax.psum(local_sums, 'qoi')]
    unnamed x4 -> x2, local copies, waits for them, and re-layouts: 0.64 us -> 2.62 us
    dot_general x3 -> x0, matrix products: 1.14 us -> none  [the longest x1 0.54 us: local(): jnp.einsum('fkcp,fpx->ckfx', spectra, weights, preferred_element_type=jnp...]
    mul x1 -> x0, other arithmetic: 0.6 us -> none  [local(): return (qoi_spectrum, summed * norm_factor)]
where the time goes in v1:
time: 26.6 us; the launch traced here: 26.2 us
  Pallas kernels  22.3 us (84%)
  local copies, waits for them, and re-layouts  2.62 us (10%)
  between operations  1.28 us (5%)
    pallas_call x1, Pallas kernels, local(): pl.pallas_call(functools.partial(kernel, param_count, qoi_count), out_sha...  22.3 us
    unnamed x2, local copies, waits for them, and re-layouts  2.62 us

profile of v1, /device:TPU:0, one launch (start us, length us, event | category | flops | bytes accessed | tf_op | source)
XLA Modules:
  0.0 26.2 jit_solution(10158570594502675698)
XLA Ops:
  1.3 22.3 %shard_map.59 = (f32[1,2,8,256]{3,2,1,0:T(8,128)}, f32[1,2,8,16]{3,2,1,0:T(8,128)}) custom-call(s32[1]{0:T(128)S(6)} %copy.8.start_hbm, s32[1,256]{1,0:T(1,128)} %bitcast.3, bf16[420,8,320]{2,1,0:T(8,128)(2,1)} %bitcast.2, bf16[8,320,2,256]{3,2,1,0:T(2,128)(2,1)} %rows_hbm.1), custom_call_target="tpu_custom_call" | custom-call | tf_op jit(solution)/shard_map/pallas_call | solution.py:252
  23.6 1.3 %copy.9 = f32[1,2,8,256]{3,2,1,0:T(8,128)} copy(f32[1,2,8,256]{3,2,1,0:T(8,128)} %get-tuple-element.4) | data formatting | bytes 32768
  25.0 1.3 %copy.10 = f32[1,2,8,16]{3,2,1,0:T(8,128)} copy(f32[1,2,8,16]{3,2,1,0:T(8,128)} %get-tuple-element.5) | data formatting | bytes 2048

commit v2 on v1

--- a/solution.py
+++ b/solution.py
@@ -36,31 +36,16 @@
     return wide.reshape(4 * freq_count * repeat, count * repeat).astype(jnp.bfloat16)
 
 
-def spread(width):
-    row = lax.broadcasted_iota(jnp.int32, (2 * width, 2 * width), 0)
-    col = lax.broadcasted_iota(jnp.int32, (2 * width, 2 * width), 1)
-    real = jnp.where(col == 2 * row, 1.0, 0.0)
-    imag = jnp.where(col == 2 * (row - width) + 1, -1.0, 0.0)
-    return jnp.where(row < width, real, imag).astype(jnp.bfloat16)
-
-
-def swap():
-    row = lax.broadcasted_iota(jnp.int32, (LANES, LANES), 0)
-    col = lax.broadcasted_iota(jnp.int32, (LANES, LANES), 1)
-    odd = col % 2
-    value = jnp.where(odd == 1, 1.0, -1.0)
-    return jnp.where(row == col + 1 - 2 * odd, value, 0.0).astype(jnp.bfloat16)
-
-
 def kernel(
-    param_count, qoi_count, start_hbm, group_ref, samples_hbm, rows_hbm,
+    param_count, qoi_count, start_hbm, group_hbm, samples_hbm, rows_hbm,
     out_ref, seg_ref,
-    start_ref, samples, weights, line, product, outgoing, incoming, total, segments,
-    start_sem, samples_sem, weights_sem, line_send, line_recv, out_send, out_recv, seg_send, seg_recv,
+    start_ref, group_ref, samples, weights, loose, dense, line, product, outgoing, incoming, total, segments,
+    start_sem, group_sem, samples_sem, weights_sem, line_send, line_recv, out_send, out_recv, seg_send, seg_recv,
 ):
     steps_count, sample_local, param_local = samples.shape
-    freq_count, halves = weights.shape[0], weights.shape[1]
-    gauge_local = halves * LANES
+    freq_count = weights.shape[0]
+    gauge_local = group_ref.shape[1]
+    halves = gauge_local // LANES
     sample_total = sample_local * qoi_count
     depth = 2 * param_local
     per_chunk = freq_count // CHUNKS
@@ -79,6 +64,8 @@
 
     start_copy = pltpu.make_async_copy(start_hbm, start_ref, start_sem)
     start_copy.start()
+    group_copy = pltpu.make_async_copy(group_hbm, group_ref, group_sem)
+    group_copy.start()
     edges = [steps_count * part // PARTS // 32 * 32 for part in range(PARTS)] + [steps_count]
     sample_copies = []
     for part in range(PARTS):
@@ -88,41 +75,31 @@
         )
         copy.start()
         sample_copies.append(copy)
-    weight_copies = []
-    for f in range(freq_count):
-        for j in range(halves):
-            copy = pltpu.make_async_copy(
-                rows_hbm.at[f, :, :, pl.ds(j * LANES, LANES)],
-                weights.at[f, j],
-                weights_sem.at[f, j],
-            )
-            copy.start()
-            weight_copies.append(copy)
-
     start_copy.wait()
     start = start_ref[0]
-    swapper = swap()
+    weight_copies = [
+        pltpu.make_async_copy(rows_hbm.at[f], weights.at[f], weights_sem.at[f])
+        for f in range(freq_count)
+    ]
     both = None
     for part in range(PARTS):
         first, count = edges[part], edges[part + 1] - edges[part]
         table = build_table(start, freq_count, steps_count, first, count, sample_local)
         sample_copies[part].wait()
+        if part == 0:
+            for copy in weight_copies:
+                copy.start()
         block = samples[pl.ds(first, count)].reshape(count * sample_local, param_local)
         term = jnp.dot(table, block, preferred_element_type=jnp.float32)
         both = term if both is None else both + term
     half = 2 * freq_count * sample_local
     spectrum = (both[:half] + both[half:]).astype(jnp.bfloat16)
-    blocks = depth // LANES
-    for base in range(0, param_local, LANES):
-        width = min(LANES, param_local - base)
-        pair = jnp.concatenate(
-            [spectrum[: half // 2, base : base + width], spectrum[half // 2 :, base : base + width]],
-            axis=1,
-        )
-        value = jnp.dot(pair, spread(width), preferred_element_type=jnp.float32)
-        line[0, :, :, 2 * base : 2 * (base + width)] = (
-            value.reshape(freq_count, sample_local, 2 * width).astype(jnp.bfloat16)
-        )
+    aligned = param_local // LANES * LANES
+    parts = [spectrum[: half // 2], spectrum[half // 2 :]]
+    pieces = [part[:, :aligned] for part in parts]
+    if aligned < param_local:
+        pieces.append(jnp.concatenate([part[:, aligned:] for part in parts], axis=1))
+    line[0] = jnp.concatenate(pieces, axis=1).reshape(freq_count, sample_local, depth)
 
     pl.semaphore_wait(barrier, qoi_count + param_count - 2)
     line_copies = []
@@ -140,33 +117,42 @@
             copy.start()
             line_copies.append(copy)
 
+    for f in range(freq_count):
+        weight_copies[f].wait()
+        loose[...] = weights[f].astype(jnp.float32)
+        for j in range(halves):
+            parts = [
+                loose[pl.ds(2 * j + part, param_local, stride=2 * halves), :].astype(jnp.bfloat16)
+                for part in range(2)
+            ]
+            dense[f, :, j * LANES : (j + 1) * LANES] = jnp.concatenate(
+                [part[:aligned] for part in parts] + [part[aligned:] for part in parts], axis=0
+            )
+
+    lane = lax.broadcasted_iota(jnp.int32, (1, depth), 1)
+    tail = param_local - aligned
+    second = ((lane >= aligned) & (lane < 2 * aligned)) | (lane >= 2 * aligned + tail)
+    sign = jnp.where(second, -1.0, 1.0)
     out_copies = []
     stripe = 2 * per_chunk
     for chunk in range(CHUNKS):
         for offset in range(1, qoi_count):
             line_copies[chunk * (qoi_count - 1) + offset - 1].wait_recv()
         for f in range(chunk * per_chunk, (chunk + 1) * per_chunk):
-            real = jnp.concatenate([line[slot, f] for slot in range(qoi_count)], axis=0)
-            stacked = jnp.concatenate(
-                [real[:, b * LANES : (b + 1) * LANES] for b in range(blocks)], axis=0
-            )
-            turned = jnp.dot(stacked, swapper, preferred_element_type=jnp.float32).astype(
-                jnp.bfloat16
-            )
-            imag = jnp.concatenate(
-                [turned[b * sample_total : (b + 1) * sample_total] for b in range(blocks)], axis=1
-            )
-            left = jnp.concatenate([real, imag], axis=0)
+            given = jnp.concatenate(
+                [line[slot, f].astype(jnp.float32) for slot in range(qoi_count)], axis=0
+            )
+            real = given * sign
+            swapped = [given[:, aligned : 2 * aligned], given[:, :aligned]]
+            if tail:
+                swapped.append(pltpu.roll(given[:, 2 * aligned :], tail, 1))
+            left = jnp.concatenate([real, jnp.concatenate(swapped, axis=1)], axis=0)
+            result = jnp.dot(
+                left.astype(jnp.bfloat16), dense[f], preferred_element_type=jnp.float32
+            )
+            rows = 2 * sample_total
             for j in range(halves):
-                weight_copies[f * halves + j].wait()
-            right = jnp.concatenate(
-                [weights[f, j].reshape(depth, LANES) for j in range(halves)], axis=1
-            )
-            result = jnp.dot(left, right, preferred_element_type=jnp.float32)
-            for j in range(halves):
-                product[j, pl.ds(f * 2 * sample_total, 2 * sample_total), :] = result[
-                    :, j * LANES : (j + 1) * LANES
-                ]
+                product[j, pl.ds(f * rows, rows), :] = result[:, j * LANES : (j + 1) * LANES]
         for r in range(sample_total):
             for j in range(halves):
                 outgoing[r, chunk, :, j * LANES : (j + 1) * LANES] = product[
@@ -189,6 +175,7 @@
             copy.start()
             out_copies.append(copy)
 
+    group_copy.wait()
     group_rows = lax.broadcasted_iota(jnp.int32, (LANES, gauge_local), 0)
     onehot = (group_rows == group_ref[...]).astype(jnp.float32)
     slot = lax.rem(me_q + qoi_count - me_p // sample_local, qoi_count)
@@ -247,8 +234,11 @@
     depth = 2 * param_local
     stripe = 2 * freq_count // CHUNKS
     assert sample_total == param_count
+    rows = operator_rows.reshape(freq_count, param_local, 2, halves, LANES)
+    rows = rows.transpose(0, 1, 3, 2, 4).reshape(freq_count, depth * halves, LANES)
     dma = pltpu.SemaphoreType.DMA
     vmem = pl.BlockSpec(memory_space=pltpu.VMEM)
+    hbm = pl.BlockSpec(memory_space=pltpu.HBM)
     return pl.pallas_call(
         functools.partial(kernel, param_count, qoi_count),
         out_shape=(
@@ -257,15 +247,18 @@
         ),
         in_specs=[
             pl.BlockSpec(memory_space=pl.ANY),
-            vmem,
-            pl.BlockSpec(memory_space=pl.ANY),
-            pl.BlockSpec(memory_space=pl.ANY),
+            hbm,
+            hbm,
+            hbm,
         ],
         out_specs=(vmem, vmem),
         scratch_shapes=[
             pltpu.SMEM((1,), jnp.int32),
+            pltpu.VMEM((1, gauge_local), jnp.int32),
             pltpu.VMEM((steps_count, sample_local, param_local), jnp.bfloat16),
-            pltpu.VMEM((freq_count, halves, param_local, 2, LANES), jnp.bfloat16),
+            pltpu.VMEM((freq_count, depth * halves, LANES), jnp.bfloat16),
+            pltpu.VMEM((depth * halves, LANES), jnp.float32),
+            pltpu.VMEM((freq_count, depth, gauge_local), jnp.bfloat16),
             pltpu.VMEM((qoi_count, freq_count, sample_local, depth), jnp.bfloat16),
             pltpu.VMEM((halves, freq_count * 2 * sample_total, LANES), jnp.float32),
             pltpu.VMEM((sample_total, CHUNKS, stripe, gauge_local), jnp.bfloat16),
@@ -273,8 +266,9 @@
             pltpu.VMEM((halves, 2 * freq_count, LANES), jnp.float32),
             pltpu.VMEM((qoi_count, 2 * freq_count, LANES), jnp.float32),
             dma(()),
+            dma(()),
             dma((PARTS,)),
-            dma((freq_count, halves)),
+            dma((freq_count,)),
             dma((CHUNKS, qoi_count)),
             dma((CHUNKS, qoi_count)),
             dma((CHUNKS, param_count)),
@@ -282,8 +276,8 @@
             dma((qoi_count,)),
             dma((qoi_count,)),
         ],
-        compiler_params=pltpu.CompilerParams(collective_id=0, has_side_effects=True),
-    )(block_start, gauge_group.reshape(1, gauge_local), samples.transpose(2, 0, 1), operator_rows)
+        compiler_params=pltpu.CompilerParams(collective_id=0, has_side_effects=True, vmem_limit_bytes=53 * 2**20),
+    )(block_start, gauge_group.reshape(1, gauge_local), samples.transpose(2, 0, 1), rows)
 
 
 def solution(mesh):

time: 26.6 us -> 21.6 us (0.81)
  Pallas kernels: 22.3 us -> 18.2 us
  local copies, waits for them, and re-layouts: 2.62 us -> 1.88 us
    pallas_call x1, Pallas kernels: 22.3 us -> 18.2 us  [local(): pl.pallas_call(functools.partial(kernel, param_count, qoi_count), out_sha...]
    unnamed x2 -> x4, local copies, waits for them, and re-layouts: 2.62 us -> 1.88 us
where the time goes in v2:
time: 21.6 us; the launch traced here: 21.4 us
  Pallas kernels  18.2 us (84%)
  local copies, waits for them, and re-layouts  1.88 us (9%)
  between operations  1.29 us (6%)
    pallas_call x1, Pallas kernels, local(): pl.pallas_call(functools.partial(kernel, param_count, qoi_count), out_sha...  18.2 us
    unnamed x4, local copies, waits for them, and re-layouts  1.88 us

profile of v2, /device:TPU:0, one launch (start us, length us, event | category | flops | bytes accessed | tf_op | source)
XLA Modules:
  0.0 21.4 jit_solution(11241353961777583874)
XLA Ops:
  1.3 0.0 copy-start
  1.3 0.7 %copy-done = s32[256]{0:T(256)S(1)} copy-done((s32[256]{0:T(256)S(1)}, s32[256]{0:T(256)}, u32[]{:S(2)}) %copy-start) | copy-done | bytes 1048
  2.0 18.2 %shard_map.59 = (f32[1,2,8,256]{3,2,1,0:T(8,128)S(1)}, f32[1,2,8,16]{3,2,1,0:T(8,128)S(1)}) custom-call(s32[1]{0:T(128)S(6)} %copy.9.start_hbm, s32[1,256]{1,0:T(1,128)S(1)} %bitcast.7, bf16[420,8,320]{2,1,0:T(8,128)(2,1)} %bitcast.9, bf16[8,1280,128]{2,1,0:T(8,128)(2,1)} %bitcast.8), custom_call_target="tpu_custom_call" | custom-call | tf_op jit(solution)/shard_map/pallas_call | solution.py:242
  20.2 0.6 %copy.10 = f32[1,2,8,256]{3,2,1,0:T(8,128)} copy(f32[1,2,8,256]{3,2,1,0:T(8,128)S(1)} %get-tuple-element.4) | data formatting | bytes 32768
  20.8 0.6 %copy.11 = f32[1,2,8,16]{3,2,1,0:T(8,128)} copy(f32[1,2,8,16]{3,2,1,0:T(8,128)S(1)} %get-tuple-element.5) | data formatting | bytes 2048
Async XLA Ops:
  1.3 0.7 %copy-start = (s32[256]{0:T(256)S(1)}, s32[256]{0:T(256)}, u32[]{:S(2)}) copy-start(s32[256]{0:T(256)} %param.7) | copy-start | bytes 3076

commit v3 on v2

--- a/solution.py
+++ b/solution.py
@@ -10,7 +10,7 @@
 
 GROUPS = 16
 LANES = 128
-CHUNKS = 2
+CHUNKS = 1
 PARTS = 2
 MESH = pl.DeviceIdType.MESH
 NT_DIMS = (((1,), (1,)), ((), ()))
@@ -39,8 +39,8 @@
 def kernel(
     param_count, qoi_count, start_hbm, group_hbm, samples_hbm, rows_hbm,
     out_ref, seg_ref,
-    start_ref, group_ref, samples, weights, loose, dense, line, product, outgoing, incoming, total, segments,
-    start_sem, group_sem, samples_sem, weights_sem, line_send, line_recv, out_send, out_recv, seg_send, seg_recv,
+    start_ref, group_ref, samples, weights, loose, dense, hot, line, product, outgoing, incoming, total, joined, shares, gathered,
+    start_sem, group_sem, samples_sem, weights_sem, line_send, line_recv, out_send, out_recv, share_send, share_recv,
 ):
     steps_count, sample_local, param_local = samples.shape
     freq_count = weights.shape[0]
@@ -53,14 +53,17 @@
     me_q = lax.axis_index("qoi")
 
     barrier = pltpu.get_barrier_semaphore()
-    for offset in range(1, qoi_count):
-        pl.semaphore_signal(
-            barrier, inc=1, device_id=(me_p, lax.rem(me_q + offset, qoi_count)), device_id_type=MESH
-        )
-    for offset in range(1, param_count):
-        pl.semaphore_signal(
-            barrier, inc=1, device_id=(lax.rem(me_p + offset, param_count), me_q), device_id_type=MESH
-        )
+    for far in range(qoi_count):
+        for offset in range(param_count):
+            if far or offset:
+                pl.semaphore_signal(
+                    barrier,
+                    inc=1,
+                    device_id=(
+                        lax.rem(me_p + offset, param_count), lax.rem(me_q + far, qoi_count)
+                    ),
+                    device_id_type=MESH,
+                )
 
     start_copy = pltpu.make_async_copy(start_hbm, start_ref, start_sem)
     start_copy.start()
@@ -99,16 +102,16 @@
     pieces = [part[:, :aligned] for part in parts]
     if aligned < param_local:
         pieces.append(jnp.concatenate([part[:, aligned:] for part in parts], axis=1))
-    line[0] = jnp.concatenate(pieces, axis=1).reshape(freq_count, sample_local, depth)
-
-    pl.semaphore_wait(barrier, qoi_count + param_count - 2)
+    line[me_q] = jnp.concatenate(pieces, axis=1).reshape(freq_count, sample_local, depth)
+
+    pl.semaphore_wait(barrier, qoi_count * param_count - 1)
     line_copies = []
     for chunk in range(CHUNKS):
         picked = pl.ds(chunk * per_chunk, per_chunk)
         for offset in range(1, qoi_count):
             copy = pltpu.make_async_remote_copy(
-                src_ref=line.at[0, picked],
-                dst_ref=line.at[offset, picked],
+                src_ref=line.at[me_q, picked],
+                dst_ref=line.at[me_q, picked],
                 send_sem=line_send.at[chunk, offset],
                 recv_sem=line_recv.at[chunk, offset],
                 device_id=(me_p, lax.rem(me_q + offset, qoi_count)),
@@ -129,11 +132,17 @@
                 [part[:aligned] for part in parts] + [part[aligned:] for part in parts], axis=0
             )
 
+    group_copy.wait()
+    columns = lax.broadcasted_iota(jnp.int32, (LANES, gauge_local), 0)
+    for f in range(freq_count):
+        hot[f] = (columns == group_ref[...] + f * GROUPS).astype(jnp.float32).astype(jnp.bfloat16)
+
     lane = lax.broadcasted_iota(jnp.int32, (1, depth), 1)
     tail = param_local - aligned
     second = ((lane >= aligned) & (lane < 2 * aligned)) | (lane >= 2 * aligned + tail)
     sign = jnp.where(second, -1.0, 1.0)
     out_copies = []
+    order = list(range(1, param_count))
     stripe = 2 * per_chunk
     for chunk in range(CHUNKS):
         for offset in range(1, qoi_count):
@@ -151,6 +160,10 @@
                 left.astype(jnp.bfloat16), dense[f], preferred_element_type=jnp.float32
             )
             rows = 2 * sample_total
+            sums = lax.dot_general(
+                result.astype(jnp.bfloat16), hot[f], NT_DIMS, preferred_element_type=jnp.float32
+            )
+            segment = sums if f == 0 else segment + sums
             for j in range(halves):
                 product[j, pl.ds(f * rows, rows), :] = result[:, j * LANES : (j + 1) * LANES]
         for r in range(sample_total):
@@ -160,12 +173,32 @@
                     pl.ds(chunk * per_chunk * 2 * sample_total + r, stripe, stride=sample_total),
                     :,
                 ].astype(jnp.bfloat16)
-        for offset in range(1, param_count):
+        if chunk == CHUNKS - 1:
+            joined[...] = segment * math.sqrt(GROUPS / (gauge_local * qoi_count))
+            for k in range(sample_total):
+                shares[k] = joined[pl.ds(k, 2, stride=sample_total), :]
+            mine = me_q * param_count + me_p
+            gathered[mine] = shares[me_p]
+            seg_copies = []
+            for far in reversed(range(qoi_count)):
+                for offset in order + [0]:
+                    if far == 0 and offset == 0:
+                        continue
+                    target = lax.rem(me_p + offset, param_count)
+                    copy = pltpu.make_async_remote_copy(
+                        src_ref=shares.at[target],
+                        dst_ref=gathered.at[mine],
+                        send_sem=share_send.at[far * param_count + offset],
+                        recv_sem=share_recv.at[far * param_count + offset],
+                        device_id=(target, lax.rem(me_q + far, qoi_count)),
+                        device_id_type=MESH,
+                    )
+                    copy.start()
+                    seg_copies.append(copy)
+        for offset in order:
             target = lax.rem(me_p + offset, param_count)
-            slot = lax.rem(me_q + qoi_count - target // sample_local, qoi_count)
-            place = slot * sample_local + lax.rem(target, sample_local)
             copy = pltpu.make_async_remote_copy(
-                src_ref=outgoing.at[place, chunk],
+                src_ref=outgoing.at[target, chunk],
                 dst_ref=incoming.at[offset, chunk],
                 send_sem=out_send.at[chunk, offset],
                 recv_sem=out_recv.at[chunk, offset],
@@ -175,15 +208,10 @@
             copy.start()
             out_copies.append(copy)
 
-    group_copy.wait()
-    group_rows = lax.broadcasted_iota(jnp.int32, (LANES, gauge_local), 0)
-    onehot = (group_rows == group_ref[...]).astype(jnp.float32)
-    slot = lax.rem(me_q + qoi_count - me_p // sample_local, qoi_count)
-    place = slot * sample_local + lax.rem(me_p, sample_local)
     for chunk in range(CHUNKS):
-        partial = outgoing[place, chunk].astype(jnp.float32)
-        for offset in range(1, param_count):
-            out_copies[chunk * (param_count - 1) + offset - 1].wait_recv()
+        partial = outgoing[me_p, chunk].astype(jnp.float32)
+        for index, offset in reversed(list(enumerate(order))):
+            out_copies[chunk * (param_count - 1) + index].wait_recv()
             partial = partial + incoming[offset, chunk].astype(jnp.float32)
         for j in range(halves):
             total[j, pl.ds(chunk * stripe, stripe), :] = partial[:, j * LANES : (j + 1) * LANES]
@@ -196,33 +224,15 @@
         ],
         axis=0,
     )
-    sums = lax.dot_general(
-        ordered, onehot, NT_DIMS, precision=lax.Precision.HIGHEST,
-        preferred_element_type=jnp.float32,
-    )
-    segments[me_q] = sums
-    seg_copies = []
-    for offset in range(1, qoi_count):
-        copy = pltpu.make_async_remote_copy(
-            src_ref=segments.at[me_q],
-            dst_ref=segments.at[me_q],
-            send_sem=seg_send.at[offset],
-            recv_sem=seg_recv.at[offset],
-            device_id=(me_p, lax.rem(me_q + offset, qoi_count)),
-            device_id_type=MESH,
-        )
-        copy.start()
-        seg_copies.append(copy)
     out_ref[...] = ordered.reshape(out_ref.shape)
     for copy in line_copies + out_copies:
         copy.wait_send()
     for copy in seg_copies:
         copy.wait()
-    everything = segments[0]
-    for q in range(1, qoi_count):
-        everything = everything + segments[q]
-    everything = everything * math.sqrt(GROUPS / (gauge_local * qoi_count))
-    seg_ref[...] = everything[:, :GROUPS].reshape(seg_ref.shape)
+    final = gathered[0]
+    for p in range(1, param_count * qoi_count):
+        final = final + gathered[p]
+    seg_ref[...] = final.reshape(seg_ref.shape)
 
 
 def local(samples, operator_rows, block_start, gauge_group):
@@ -233,17 +243,17 @@
     halves = gauge_local // LANES
     depth = 2 * param_local
     stripe = 2 * freq_count // CHUNKS
-    assert sample_total == param_count
+    assert sample_total == param_count and freq_count * GROUPS == LANES
     rows = operator_rows.reshape(freq_count, param_local, 2, halves, LANES)
     rows = rows.transpose(0, 1, 3, 2, 4).reshape(freq_count, depth * halves, LANES)
     dma = pltpu.SemaphoreType.DMA
     vmem = pl.BlockSpec(memory_space=pltpu.VMEM)
     hbm = pl.BlockSpec(memory_space=pltpu.HBM)
-    return pl.pallas_call(
+    qoi_spectrum, response = pl.pallas_call(
         functools.partial(kernel, param_count, qoi_count),
         out_shape=(
             jax.ShapeDtypeStruct((1, 2, freq_count, gauge_local), jnp.float32),
-            jax.ShapeDtypeStruct((1, 2, freq_count, GROUPS), jnp.float32),
+            jax.ShapeDtypeStruct((1, 2, freq_count * GROUPS), jnp.float32),
         ),
         in_specs=[
             pl.BlockSpec(memory_space=pl.ANY),
@@ -259,12 +269,15 @@
             pltpu.VMEM((freq_count, depth * halves, LANES), jnp.bfloat16),
             pltpu.VMEM((depth * halves, LANES), jnp.float32),
             pltpu.VMEM((freq_count, depth, gauge_local), jnp.bfloat16),
+            pltpu.VMEM((freq_count, LANES, gauge_local), jnp.bfloat16),
             pltpu.VMEM((qoi_count, freq_count, sample_local, depth), jnp.bfloat16),
             pltpu.VMEM((halves, freq_count * 2 * sample_total, LANES), jnp.float32),
             pltpu.VMEM((sample_total, CHUNKS, stripe, gauge_local), jnp.bfloat16),
             pltpu.VMEM((param_count, CHUNKS, stripe, gauge_local), jnp.bfloat16),
             pltpu.VMEM((halves, 2 * freq_count, LANES), jnp.float32),
-            pltpu.VMEM((qoi_count, 2 * freq_count, LANES), jnp.float32),
+            pltpu.VMEM((2 * sample_total, LANES), jnp.float32),
+            pltpu.VMEM((sample_total, 2, LANES), jnp.float32),
+            pltpu.VMEM((qoi_count * param_count, 2, LANES), jnp.float32),
             dma(()),
             dma(()),
             dma((PARTS,)),
@@ -273,11 +286,12 @@
             dma((CHUNKS, qoi_count)),
             dma((CHUNKS, param_count)),
             dma((CHUNKS, param_count)),
-            dma((qoi_count,)),
-            dma((qoi_count,)),
+            dma((qoi_count * param_count,)),
+            dma((qoi_count * param_count,)),
         ],
         compiler_params=pltpu.CompilerParams(collective_id=0, has_side_effects=True, vmem_limit_bytes=53 * 2**20),
     )(block_start, gauge_group.reshape(1, gauge_local), samples.transpose(2, 0, 1), rows)
+    return qoi_spectrum, response.reshape(1, 2, freq_count, GROUPS)
 
 
 def solution(mesh):

time: 21.6 us -> 20.5 us (0.949)
  Pallas kernels: 18.2 us -> 17 us
    pallas_call x1, Pallas kernels: 18.2 us -> 17 us  [local(): pl.pallas_call(functools.partial(kernel, param_count, qoi_count), out_sha...]
    reshape x0 -> x1, local copies, waits for them, and re-layouts: none -> 0.68 us  [local(): return (qoi_spectrum, response.reshape(1, 2, freq_count, GROUPS))]
    unnamed x4 -> x3, local copies, waits for them, and re-layouts: 1.88 us -> 1.28 us
where the time goes in v3:
time: 20.5 us; the launch traced here: 20.3 us
  Pallas kernels  17 us (83%)
  local copies, waits for them, and re-layouts  1.96 us (10%)
  between operations  1.29 us (6%)
    pallas_call x1, Pallas kernels, local(): pl.pallas_call(functools.partial(kernel, param_count, qoi_count), out_sha...  17 us
    unnamed x3, local copies, waits for them, and re-layouts  1.28 us
    reshape x1, local copies, waits for them, and re-layouts, local(): return (qoi_spectrum, response.reshape(1, 2, freq_count, GROUPS))  0.68 us

profile of v3, /device:TPU:0, one launch (start us, length us, event | category | flops | bytes accessed | tf_op | source)
XLA Modules:
  0.0 20.3 jit_solution(11532010931568962464)
XLA Ops:
  1.3 0.0 copy-start
  1.3 0.7 %copy-done = s32[256]{0:T(256)S(1)} copy-done((s32[256]{0:T(256)S(1)}, s32[256]{0:T(256)}, u32[]{:S(2)}) %copy-start) | copy-done | bytes 1048
  2.0 17.0 %shard_map.59 = (f32[1,2,8,256]{3,2,1,0:T(8,128)S(1)}, f32[1,2,128]{2,1,0:T(2,128)S(1)}) custom-call(s32[1]{0:T(128)S(6)} %copy.8.start_hbm, s32[1,256]{1,0:T(1,128)S(1)} %bitcast.7, bf16[420,8,320]{2,1,0:T(8,128)(2,1)} %bitcast.9, bf16[8,1280,128]{2,1,0:T(8,128)(2,1)} %bitcast.8), custom_call_target="tpu_custom_call" | custom-call | tf_op jit(solution)/shard_map/pallas_call | solution.py:252
  19.0 0.7 %reshape.19 = f32[1,2,8,16]{3,2,1,0:T(8,128)} reshape(f32[1,2,128]{2,1,0:T(2,128)S(1)} %get-tuple-element.5) | data formatting | bytes 2048 | tf_op jit(solution)/shard_map/reshape | solution.py:294
  19.7 0.6 %copy.9 = f32[1,2,8,256]{3,2,1,0:T(8,128)} copy(f32[1,2,8,256]{3,2,1,0:T(8,128)S(1)} %get-tuple-element.8) | data formatting | bytes 32768
Async XLA Ops:
  1.3 0.7 %copy-start = (s32[256]{0:T(256)S(1)}, s32[256]{0:T(256)}, u32[]{:S(2)}) copy-start(s32[256]{0:T(256)} %param.7) | copy-start | bytes 3076
